TPU v7x, 32 devices: a whole 2x2x4 slice. The times are simulated.
32 devices in a mesh: lat: 16 (over z, y, core), lon: 2 (over x).
Axes of the slice: x: 2, y: 2, z: 4, core: 2. Of those that a mesh axis runs over, the one named last changes fastest.
Arguments:
- features: bfloat16 [256, 128, 512], P('lat', 'lon'), may hold values from -6 to 6
- upstream: bfloat16 [256, 128, 512], P('lat', 'lon'), may hold values from -6 to 6
- kernel: bfloat16 [4608, 512], replicated, may hold values from -0.09375 to 0.09375
Outputs:
- input_grad: bfloat16 [256, 128, 512], P('lat', 'lon')
- direction: float32 [4608, 512], P('lat')
- perturbed: float32 [4608, 512], P('lat')
All inputs are finite; a program needn't handle non-finite values.
Results may differ from a plain program's by a relative error of at most 0.0032.
Values may be sent and summed in bfloat16 or wider, within the bound.
A program may use at most 128 MiB of HBM per device.

v0:
```python
import jax
import jax.numpy as jnp
from jax import lax
from jax.sharding import PartitionSpec as P


def padded_2(block, sides, width, periodic):
    for axis, dim in sides:
        count = lax.axis_size(axis)
        forward = [(i, i + 1) for i in range(count - 1)]
        if periodic:
            forward.append((count - 1, 0))
        backward = [(target, source) for source, target in forward]
        low = lax.ppermute(
            lax.slice_in_dim(block, block.shape[dim] - width, None, axis=dim), axis, forward
        )
        high = lax.ppermute(lax.slice_in_dim(block, 0, width, axis=dim), axis, backward)
        block = jnp.concatenate([low, block, high], axis=dim)
    return block


def convolve(padded, kernel, height, breadth):
    channels = kernel.shape[1]
    total = jnp.zeros((height, breadth, channels), jnp.float32)
    for a in range(3):
        for b in range(3):
            t = 3 * a + b
            total = total + jnp.dot(
                padded[a : a + height, b : b + breadth],
                kernel[t * channels : (t + 1) * channels],
                preferred_element_type=jnp.float32,
            )
    return total


def spread(padded, kernel, height, breadth):
    channels = kernel.shape[1]
    total = jnp.zeros((height, breadth, channels), jnp.float32)
    for a in range(3):
        for b in range(3):
            t = 3 * a + b
            piece = padded[2 - a : 2 - a + height, 2 - b : 2 - b + breadth]
            total = total + lax.dot_general(
                piece,
                kernel[t * channels : (t + 1) * channels],
                (((2,), (1,)), ((), ())),
                preferred_element_type=jnp.float32,
            )
    return total


def weight_terms(padded, slope, height, breadth):
    blocks = []
    for a in range(3):
        for b in range(3):
            blocks.append(
                lax.dot_general(
                    padded[a : a + height, b : b + breadth],
                    slope,
                    (((0, 1), (0, 1)), ((), ())),
                    preferred_element_type=jnp.float32,
                )
            )
    return jnp.concatenate(blocks, axis=0)


def gated(upstream, z):
    sig = jax.nn.sigmoid(z)
    return upstream.astype(jnp.float32) * sig * (1.0 + z * (1.0 - sig))


def shards(features, upstream, kernel):
    height, breadth, channels = features.shape
    wide_cols = padded_2(features, (("lon", 1),), 1, True)
    padded_x = padded_2(wide_cols, (("lat", 0),), 1, False)
    z = convolve(padded_x, kernel, height, breadth)
    slope = gated(upstream, z).astype(jnp.bfloat16)
    slope_cols = padded_2(slope, (("lon", 1),), 1, True)
    padded_slope = padded_2(slope_cols, (("lat", 0),), 1, False)
    back = upstream.astype(jnp.float32) + spread(padded_slope, kernel, height, breadth)
    input_grad = back.astype(jnp.bfloat16)
    local_grad = weight_terms(padded_x, slope, height, breadth)
    row_block = lax.psum_scatter(local_grad, "lat", scatter_dimension=0, tiled=True)
    summed = lax.psum(row_block, "lon")
    total = lax.psum(jnp.sum(summed * summed), "lat")
    count = 9.0 * channels * channels
    direction = summed / jnp.sqrt(total / count + 1e-06)
    block_rows = summed.shape[0]
    start = lax.axis_index("lat") * block_rows
    own_kernel = lax.dynamic_slice_in_dim(kernel, start, block_rows, 0)
    perturbed = own_kernel.astype(jnp.float32) + 0.05 / jnp.sqrt(count) * direction
    return (input_grad, direction, perturbed)


def solution(mesh):
    return jax.shard_map(
        shards,
        mesh=mesh,
        in_specs=(P("lat", "lon", None), P("lat", "lon", None), P()),
        out_specs=(P("lat", "lon", None), P("lat", None), P("lat", None)),
        check_vma=False,
    )
```

profile of v0, /device:TPU:0, one launch (start us, length us, event | category | flops | bytes accessed | tf_op | source)
XLA Modules:
  0.0 243.8 jit_solution(826851262055394935)
XLA Ops:
  8.3 3.0 %collective-permute-start = (bf16[16,1,512]{2,1,0:T(2,128)(2,1)S(1)}, bf16[16,1,512]{2,1,0:T(2,128)(2,1)S(1)}, u32[]{:S(2)}, u32[]{:S(2)}) collective-permute-start(bf16[16,1,512]{2,1,0:T(2,128)(2,1)S(1)} %get-tuple-element.15), channel_id=1, source_target_pairs={{0,1},{1,0},{2,3},{3,2},{4,5},{5,4},{6,7},{7,6},{8,9},{9,8},{10,11... | collective-permute-start | bytes 49160 | tf_op jit(solution)/shard_map/ppermute | solution.py:14
  11.4 2.1 fusion.62
  13.5 1.8 collective-permute-done.1
  15.3 1.6 collective-permute-start.2
  16.9 1.3 collective-permute-start.3
  18.2 1.8 fusion.50
  26.6 1.8 fusion.1
  28.4 1.7 fusion.11
  30.1 1.7 fusion.10
  31.8 1.7 fusion.9
  33.6 1.8 fusion.8
  35.3 1.7 fusion.7
  37.1 1.8 fusion.6
  38.8 1.7 fusion.5
  40.5 1.8 fusion.4
  42.3 1.8 fusion.3
  44.9 1.5 collective-permute-start.4
  46.4 1.8 fusion.60
  50.1 4.4 %collective-permute-start.7 = (bf16[1,66,512]{2,1,0:T(8,128)(2,1)S(1)}, bf16[1,66,512]{2,1,0:T(8,128)(2,1)S(1)}, u32[]{:S(2)}, u32[]{:S(2)}) collective-permute-start(bf16[1,66,512]{2,1,0:T(8,128)(2,1)S(1)} %get-tuple-element.8), channel_id=1, source_target_pairs={{0,2},{2,4},{4,6},{6,8},{8,10},{10,12},{12,14},{14,16},{16,18},{18... | collective-permute-start | bytes 202760 | tf_op jit(solution)/shard_map/ppermute | solution.py:14
  54.5 3.3 %fusion.22 = f32[16,64,512]{2,1,0:T(8,128)} fusion(bf16[16,1,512]{2,1,0:T(2,128)(2,1)S(1)} %collective-permute-done.5, bf16[16,64,512]{2,1,0:T(8,128)(2,1)S(1)} %fusion.1, bf16[4608,512]{1,0:T(8,128)(2,1)} %param.5), kind=kOutput, calls=%fused_computation.37 | convolution fusion | flops 538968064 | bytes 3686400 | tf_op jit(solution)/shard_map/dot_general | solution.py:43
  57.9 3.1 %fusion.20 = f32[16,64,512]{2,1,0:T(8,128)} fusion(bf16[16,64,512]{2,1,0:T(8,128)(2,1)S(1)} %fusion.1, bf16[16,1,512]{2,1,0:T(2,128)(2,1)S(1)} %collective-permute-done.4, bf16[4608,512]{1,0:T(8,128)(2,1)} %param.5), kind=kOutput, calls=%fused_computation.34 | convolution fusion | flops 538968064 | bytes 3686400 | tf_op jit(solution)/shard_map/dot_general | solution.py:43
  61.8 3.6 %fusion.16 = f32[16,64,512]{2,1,0:T(8,128)} fusion(bf16[17,66,512]{2,1,0:T(8,128)(2,1)S(1)} %get-tuple-element.6, bf16[4608,512]{1,0:T(8,128)(2,1)} %param.5), kind=kOutput, calls=%fused_computation.29 | convolution fusion | flops 536870912 | bytes 3670016 | tf_op jit(solution)/shard_map/dot_general | solution.py:43
  65.4 3.2 %fusion.18 = f32[16,64,512]{2,1,0:T(8,128)} fusion(bf16[17,66,512]{2,1,0:T(8,128)(2,1)S(1)} %get-tuple-element.6, bf16[4608,512]{1,0:T(8,128)(2,1)} %param.5), kind=kOutput, calls=%fused_computation.31 | convolution fusion | flops 536870912 | bytes 3670016 | tf_op jit(solution)/shard_map/dot_general | solution.py:43
  68.5 3.2 %fusion.24 = f32[16,64,512]{2,1,0:T(8,128)} fusion(bf16[17,66,512]{2,1,0:T(8,128)(2,1)S(1)} %get-tuple-element.5, bf16[4608,512]{1,0:T(8,128)(2,1)} %param.5), kind=kOutput, calls=%fused_computation.39 | convolution fusion | flops 536870912 | bytes 3670016 | tf_op jit(solution)/shard_map/dot_general | solution.py:43
  71.7 86.7 %reduce-scatter.2.cloned.1.call-done = f32[288,512]{1,0:T(8,128)} async-done(((f32[4608,512]{1,0:T(8,128)}), f32[288,512]{1,0:T(8,128)}) %reduce-scatter.2.cloned.1.call-update) | async-done | bytes 589840 | tf_op jit(solution)/shard_map/reduce_scatter | solution.py:83
  158.4 3.6 %fusion.26 = f32[16,64,512]{2,1,0:T(8,128)} fusion(bf16[17,66,512]{2,1,0:T(8,128)(2,1)} %copy-done.2, bf16[4608,512]{1,0:T(8,128)(2,1)} %param.5), kind=kOutput, calls=%fused_computation.41 | convolution fusion | flops 536870912 | bytes 3670016 | tf_op jit(solution)/shard_map/dot_general | solution.py:43
  162.0 3.2 %fusion.28 = f32[16,64,512]{2,1,0:T(8,128)} fusion(bf16[17,66,512]{2,1,0:T(8,128)(2,1)S(1)} %copy-done.3, bf16[4608,512]{1,0:T(8,128)(2,1)} %param.5), kind=kOutput, calls=%fused_computation.43 | convolution fusion | flops 536870912 | bytes 3670016 | tf_op jit(solution)/shard_map/dot_general | solution.py:43
  165.2 25.2 %all-reduce.2.cloned.1.call-done = f32[288,512]{1,0:T(8,128)} async-done(((f32[288,512]{1,0:T(8,128)}), f32[288,512]{1,0:T(8,128)}) %all-reduce.2.cloned.1.call-update) | async-done | bytes 589840 | tf_op jit(solution)/shard_map/psum | solution.py:84
  190.5 1.8 multiply_reduce_fusion
  192.3 7.9 %fusion.2 = bf16[16,64,512]{2,1,0:T(8,128)(2,1)} fusion(bf16[16,64,512]{2,1,0:T(8,128)(2,1)S(1)} %copy-done.5, f32[16,64,512]{2,1,0:T(8,128)} %fusion.16, f32[16,64,512]{2,1,0:T(8,128)} %fusion.18, f32[16,64,512]{2,1,0:T(8,128)} %fusion.20, f32[16,64,512]{2,1,0:T(8,128)S(1)} %fusion.60, f32[16,64,512]{2,1,0:T(8,128)} %fusion.22, f32[16,64,512]{2,1,0:T(8,128)} %fusion.24, ...), kind=kOutput, calls=%fused_computation.4 | convolution fusion | flops 542638080 | bytes 20447232 | tf_op jit(solution)/shard_map/dot_general | solution.py:43
  200.2 33.7 %psum.15 = f32[]{:T(128)} all-reduce(f32[]{:T(128)} %multiply_reduce_fusion), channel_id=1, replica_groups=mesh['lat'=16,'lon'=2] {'lat'}, use_global_device_ids=true, to_apply=%region_3.0 | all-reduce | flops 1 | bytes 8 | tf_op jit(solution)/shard_map/psum | solution.py:85
  234.6 2.3 multiply_add_fusion
  (40 shorter events, 11.4 us)
Async XLA Ops:
  7.2 8.1 %copy-start = (bf16[16,64,512]{2,1,0:T(8,128)(2,1)S(1)}, bf16[16,64,512]{2,1,0:T(8,128)(2,1)}, u32[]{:S(2)}) copy-start(bf16[16,64,512]{2,1,0:T(8,128)(2,1)} %param.3) | copy-start | bytes 3145732
  7.2 151.2 %reduce-scatter.2.cloned.1.call-start = ((), (), s32[]{:S(2)}) async-start(), calls=%async_computation.1 | async-start | bytes 10027008 | tf_op jit(solution)/shard_map/reduce_scatter | solution.py:83
  8.3 5.2 %collective-permute-start = (bf16[16,1,512]{2,1,0:T(2,128)(2,1)S(1)}, bf16[16,1,512]{2,1,0:T(2,128)(2,1)S(1)}, u32[]{:S(2)}, u32[]{:S(2)}) collective-permute-start(bf16[16,1,512]{2,1,0:T(2,128)(2,1)S(1)} %get-tuple-element.15), channel_id=1, source_target_pairs={{0,1},{1,0},{2,3},{3,2},{4,5},{5,4},{6,7},{7,6},{8,9},{9,8},{10,11... | collective-permute-start | bytes 49160 | tf_op jit(solution)/shard_map/ppermute | solution.py:14
  11.4 3.9 %collective-permute-start.1 = (bf16[16,1,512]{2,1,0:T(2,128)(2,1)S(1)}, bf16[16,1,512]{2,1,0:T(2,128)(2,1)S(1)}, u32[]{:S(2)}, u32[]{:S(2)}) collective-permute-start(bf16[16,1,512]{2,1,0:T(2,128)(2,1)S(1)} %get-tuple-element.16), channel_id=1, source_target_pairs={{1,0},{0,1},{3,2},{2,3},{5,4},{4,5},{7,6},{6,7},{9,8},{8,9},{11,10... | collective-permute-start | bytes 49160 | tf_op jit(solution)/shard_map/ppermute | solution.py:17
  15.3 4.7 %copy-start.6 = (bf16[4608,512]{1,0:T(8,128)(2,1)S(1)}, bf16[4608,512]{1,0:T(8,128)(2,1)}, u32[]{:S(2)}) copy-start(bf16[4608,512]{1,0:T(8,128)(2,1)} %param.5) | copy-start | bytes 14155780
  15.3 5.4 %collective-permute-start.2 = (bf16[1,66,512]{2,1,0:T(8,128)(2,1)S(1)}, bf16[1,66,512]{2,1,0:T(8,128)(2,1)S(1)}, u32[]{:S(2)}, u32[]{:S(2)}) collective-permute-start(bf16[1,66,512]{2,1,0:T(8,128)(2,1)S(1)} %get-tuple-element.11), channel_id=1, source_target_pairs={{0,2},{2,4},{4,6},{6,8},{8,10},{10,12},{12,14},{14,16},{16,18},{18... | collective-permute-start | bytes 202760 | tf_op jit(solution)/shard_map/ppermute | solution.py:14
  16.9 4.9 %collective-permute-start.3 = (bf16[1,66,512]{2,1,0:T(8,128)(2,1)S(1)}, bf16[1,66,512]{2,1,0:T(8,128)(2,1)S(1)}, u32[]{:S(2)}, u32[]{:S(2)}) collective-permute-start(bf16[1,66,512]{2,1,0:T(8,128)(2,1)S(1)} %get-tuple-element.12), channel_id=1, source_target_pairs={{2,0},{4,2},{6,4},{8,6},{10,8},{12,10},{14,12},{16,14},{18,16},{20... | collective-permute-start | bytes 202760 | tf_op jit(solution)/shard_map/ppermute | solution.py:17
  25.4 1.2 copy-start.4
  44.2 146.3 %all-reduce.2.cloned.1.call-start = ((), (), s32[]{:S(2)}) async-start(), calls=%async_computation.2 | async-start | bytes 1179648 | tf_op jit(solution)/shard_map/psum | solution.py:84
  44.3 4.0 %collective-permute-start.5 = (bf16[16,1,512]{2,1,0:T(2,128)(2,1)S(1)}, bf16[16,1,512]{2,1,0:T(2,128)(2,1)S(1)}, u32[]{:S(2)}, u32[]{:S(2)}) collective-permute-start(bf16[16,1,512]{2,1,0:T(2,128)(2,1)S(1)} %get-tuple-element.14), channel_id=1, source_target_pairs={{1,0},{0,1},{3,2},{2,3},{5,4},{4,5},{7,6},{6,7},{9,8},{8,9},{11,10... | collective-permute-start | bytes 49160 | tf_op jit(solution)/shard_map/ppermute | solution.py:17
  44.9 3.9 %collective-permute-start.4 = (bf16[16,1,512]{2,1,0:T(2,128)(2,1)S(1)}, bf16[16,1,512]{2,1,0:T(2,128)(2,1)S(1)}, u32[]{:S(2)}, u32[]{:S(2)}) collective-permute-start(bf16[16,1,512]{2,1,0:T(2,128)(2,1)S(1)} %get-tuple-element.13), channel_id=1, source_target_pairs={{0,1},{1,0},{2,3},{3,2},{4,5},{5,4},{6,7},{7,6},{8,9},{9,8},{10,11... | collective-permute-start | bytes 49160 | tf_op jit(solution)/shard_map/ppermute | solution.py:14
  48.8 12.2 %collective-permute-start.6 = (bf16[1,66,512]{2,1,0:T(8,128)(2,1)S(1)}, bf16[1,66,512]{2,1,0:T(8,128)(2,1)S(1)}, u32[]{:S(2)}, u32[]{:S(2)}) collective-permute-start(bf16[1,66,512]{2,1,0:T(8,128)(2,1)S(1)} %get-tuple-element.7), channel_id=1, source_target_pairs={{2,0},{4,2},{6,4},{8,6},{10,8},{12,10},{14,12},{16,14},{18,16},{20... | collective-permute-start | bytes 202760 | tf_op jit(solution)/shard_map/ppermute | solution.py:17
  50.1 10.9 %collective-permute-start.7 = (bf16[1,66,512]{2,1,0:T(8,128)(2,1)S(1)}, bf16[1,66,512]{2,1,0:T(8,128)(2,1)S(1)}, u32[]{:S(2)}, u32[]{:S(2)}) collective-permute-start(bf16[1,66,512]{2,1,0:T(8,128)(2,1)S(1)} %get-tuple-element.8), channel_id=1, source_target_pairs={{0,2},{2,4},{4,6},{6,8},{8,10},{10,12},{12,14},{14,16},{16,18},{18... | collective-permute-start | bytes 202760 | tf_op jit(solution)/shard_map/ppermute | solution.py:14
  61.8 6.8 %copy-start.1 = (bf16[17,66,512]{2,1,0:T(8,128)(2,1)}, bf16[17,66,512]{2,1,0:T(8,128)(2,1)S(1)}, u32[]{:S(2)}) copy-start(bf16[17,66,512]{2,1,0:T(8,128)(2,1)S(1)} %get-tuple-element.6) | copy-start | bytes 3446788
  61.8 6.8 %copy-start.2 = (bf16[17,66,512]{2,1,0:T(8,128)(2,1)}, bf16[17,66,512]{2,1,0:T(8,128)(2,1)S(1)}, u32[]{:S(2)}) copy-start(bf16[17,66,512]{2,1,0:T(8,128)(2,1)S(1)} %get-tuple-element.5) | copy-start | bytes 3446788
  158.4 3.6 %copy-start.3 = (bf16[17,66,512]{2,1,0:T(8,128)(2,1)S(1)}, bf16[17,66,512]{2,1,0:T(8,128)(2,1)}, u32[]{:S(2)}) copy-start(bf16[17,66,512]{2,1,0:T(8,128)(2,1)} %copy-done.2) | copy-start | bytes 3446788
  162.0 30.3 %copy-start.5 = (bf16[16,64,512]{2,1,0:T(8,128)(2,1)S(1)}, bf16[16,64,512]{2,1,0:T(8,128)(2,1)}, u32[]{:S(2)}) copy-start(bf16[16,64,512]{2,1,0:T(8,128)(2,1)} %param.4) | copy-start | bytes 3145732
Sparse Core Ops, SparseCore 0:
  44.3 114.0 reduce-scatter.1
  160.7 29.7 all-reduce.1
where the time goes:
time: 244 us
  waiting for transfers between devices  115 us (47%)
  matrix products  58.5 us (24%)
  blocking collectives  33.7 us (14%)
  between operations  14.9 us (6%)
  starting transfers between devices  13.8 us (6%)
  other arithmetic  5.77 us (2%)
    reduce_scatter x1, waiting for transfers between devices, shards(): lax.psum_scatter(local_grad, 'lat', scatter_dimension=0, tiled=True)  86.7 us
    psum x1, blocking collectives, shards(): total = lax.psum(jnp.sum(summed * summed), 'lat')  33.7 us
    dot_general x9, matrix products, spread(): lax.dot_general(piece, kernel[t * channels:(t + 1) * channels], (((2,), (...  32.9 us
    psum x1, waiting for transfers between devices, shards(): summed = lax.psum(row_block, 'lon')  25.2 us
    dot_general x9, matrix products, weight_terms(): lax.dot_general(padded[a:a + height, b:b + breadth], slope, (((0, 1), (0,...  15.7 us
    ppermute x4, starting transfers between devices, padded_2(): lax.ppermute(lax.slice_in_dim(block, block.shape[dim] - width, None, axis...  10.5 us
    dot_general x9, matrix products, convolve(): jnp.dot(padded[a:a + height, b:b + breadth], kernel[t * channels:(t + 1)...  9.83 us
  transfers between devices with their start and end apart: 10, of which 6 were waited for; matrix products, arithmetic and copies ran while one was open for 12% of the time, Pallas kernels for 0%

commit v1 on v0

--- a/solution.py
+++ b/solution.py
@@ -81,7 +81,7 @@
     input_grad = back.astype(jnp.bfloat16)
     local_grad = weight_terms(padded_x, slope, height, breadth)
     row_block = lax.psum_scatter(local_grad, "lat", scatter_dimension=0, tiled=True)
-    summed = lax.psum(row_block, "lon")
+    summed = jnp.sum(lax.all_gather(row_block, "lon"), axis=0)
     total = lax.psum(jnp.sum(summed * summed), "lat")
     count = 9.0 * channels * channels
     direction = summed / jnp.sqrt(total / count + 1e-06)

time: 244 us -> 237 us (0.971)
  waiting for transfers between devices: 115 us -> 106 us
    psum x1 -> x0, waiting for transfers between devices: 25.2 us -> none  [shards(): summed = lax.psum(row_block, 'lon')]
    all_gather x0 -> x1, waiting for transfers between devices: none -> 11 us  [shards(): summed = jnp.sum(lax.all_gather(row_block, 'lon'), axis=0)]
    reduce_scatter x1, waiting for transfers between devices: 86.7 us -> 91.4 us  [shards(): lax.psum_scatter(local_grad, 'lat', scatter_dimension=0, tiled=True)]
  transfers between devices with their start and end apart: 10 -> 10, of which waited for: 6 -> 6; matrix products, arithmetic and copies ran while one was open for 12% -> 13% of each run, Pallas kernels for 0% -> 0%
where the time goes in v1:
time: 237 us; the launch traced here: 236 us
  waiting for transfers between devices  106 us (45%)
  matrix products  58.2 us (25%)
  blocking collectives  33.7 us (14%)
  between operations  14.9 us (6%)
  starting transfers between devices  13.8 us (6%)
  other arithmetic  6.97 us (3%)
  local copies, waits for them, and re-layouts  2.74 us (1%)
    reduce_scatter x1, waiting for transfers between devices, shards(): lax.psum_scatter(local_grad, 'lat', scatter_dimension=0, tiled=True)  91.4 us
    psum x1, blocking collectives, shards(): total = lax.psum(jnp.sum(summed * summed), 'lat')  33.7 us
    dot_general x9, matrix products, spread(): lax.dot_general(piece, kernel[t * channels:(t + 1) * channels], (((2,), (...  32.6 us
    dot_general x9, matrix products, weight_terms(): lax.dot_general(padded[a:a + height, b:b + breadth], slope, (((0, 1), (0,...  15.7 us
    all_gather x1, waiting for transfers between devices, shards(): summed = jnp.sum(lax.all_gather(row_block, 'lon'), axis=0)  11 us
    ppermute x4, starting transfers between devices, padded_2(): lax.ppermute(lax.slice_in_dim(block, block.shape[dim] - width, None, axis...  10.5 us
    dot_general x9, matrix products, convolve(): jnp.dot(padded[a:a + height, b:b + breadth], kernel[t * channels:(t + 1)...  9.83 us
  transfers between devices with their start and end apart: 10, of which 6 were waited for; matrix products, arithmetic and copies ran while one was open for 13% of the time, Pallas kernels for 0%

profile of v1, /device:TPU:0, one launch (start us, length us, event | category | flops | bytes accessed | tf_op | source)
XLA Modules:
  0.0 236.1 jit_solution(14578723590189154538)
XLA Ops:
  8.3 3.0 %collective-permute-start = (bf16[16,1,512]{2,1,0:T(2,128)(2,1)S(1)}, bf16[16,1,512]{2,1,0:T(2,128)(2,1)S(1)}, u32[]{:S(2)}, u32[]{:S(2)}) collective-permute-start(bf16[16,1,512]{2,1,0:T(2,128)(2,1)S(1)} %get-tuple-element.15), channel_id=1, source_target_pairs={{0,1},{1,0},{2,3},{3,2},{4,5},{5,4},{6,7},{7,6},{8,9},{9,8},{10,11... | collective-permute-start | bytes 49160 | tf_op jit(solution)/shard_map/ppermute | solution.py:14
  11.4 2.1 fusion.62
  13.5 1.8 collective-permute-done.1
  15.3 1.6 collective-permute-start.2
  18.2 1.8 fusion.50
  26.6 1.8 fusion.1
  28.4 1.7 fusion.11
  30.1 1.7 fusion.10
  31.9 1.7 fusion.9
  33.6 1.7 fusion.8
  35.3 1.7 fusion.7
  37.0 1.8 fusion.6
  38.8 1.7 fusion.5
  40.5 1.8 fusion.4
  42.3 1.8 fusion.3
  44.8 1.5 collective-permute-start.4
  46.3 1.8 fusion.60
  50.1 4.4 %collective-permute-start.7 = (bf16[1,66,512]{2,1,0:T(8,128)(2,1)S(1)}, bf16[1,66,512]{2,1,0:T(8,128)(2,1)S(1)}, u32[]{:S(2)}, u32[]{:S(2)}) collective-permute-start(bf16[1,66,512]{2,1,0:T(8,128)(2,1)S(1)} %get-tuple-element.8), channel_id=1, source_target_pairs={{0,2},{2,4},{4,6},{6,8},{8,10},{10,12},{12,14},{14,16},{16,18},{18... | collective-permute-start | bytes 202760 | tf_op jit(solution)/shard_map/ppermute | solution.py:14
  54.5 3.3 %fusion.22 = f32[16,64,512]{2,1,0:T(8,128)} fusion(bf16[16,1,512]{2,1,0:T(2,128)(2,1)S(1)} %collective-permute-done.5, bf16[16,64,512]{2,1,0:T(8,128)(2,1)S(1)} %fusion.1, bf16[4608,512]{1,0:T(8,128)(2,1)} %param.5), kind=kOutput, calls=%fused_computation.37 | convolution fusion | flops 538968064 | bytes 3686400 | tf_op jit(solution)/shard_map/dot_general | solution.py:43
  57.8 3.1 %fusion.20 = f32[16,64,512]{2,1,0:T(8,128)} fusion(bf16[16,64,512]{2,1,0:T(8,128)(2,1)S(1)} %fusion.1, bf16[16,1,512]{2,1,0:T(2,128)(2,1)S(1)} %collective-permute-done.4, bf16[4608,512]{1,0:T(8,128)(2,1)} %param.5), kind=kOutput, calls=%fused_computation.34 | convolution fusion | flops 538968064 | bytes 3686400 | tf_op jit(solution)/shard_map/dot_general | solution.py:43
  61.0 1.8 pad_maximum_fusion.1
  63.8 3.2 %fusion.16 = f32[16,64,512]{2,1,0:T(8,128)} fusion(bf16[17,66,512]{2,1,0:T(8,128)(2,1)S(1)} %get-tuple-element.6, bf16[4608,512]{1,0:T(8,128)(2,1)} %param.5), kind=kOutput, calls=%fused_computation.29 | convolution fusion | flops 536870912 | bytes 3670016 | tf_op jit(solution)/shard_map/dot_general | solution.py:43
  67.0 91.4 %reduce-scatter.2.cloned.1.call-done = f32[288,512]{1,0:T(8,128)} async-done(((f32[4608,512]{1,0:T(8,128)}), f32[288,512]{1,0:T(8,128)}) %reduce-scatter.2.cloned.1.call-update) | async-done | bytes 589840 | tf_op jit(solution)/shard_map/reduce_scatter | solution.py:83
  158.4 3.6 %fusion.18 = f32[16,64,512]{2,1,0:T(8,128)} fusion(bf16[17,66,512]{2,1,0:T(8,128)(2,1)} %copy-done.1, bf16[4608,512]{1,0:T(8,128)(2,1)} %param.5), kind=kOutput, calls=%fused_computation.31 | convolution fusion | flops 536870912 | bytes 3670016 | tf_op jit(solution)/shard_map/dot_general | solution.py:43
  162.0 3.1 %fusion.24 = f32[16,64,512]{2,1,0:T(8,128)} fusion(bf16[17,66,512]{2,1,0:T(8,128)(2,1)S(1)} %copy-done.2, bf16[4608,512]{1,0:T(8,128)(2,1)} %param.5), kind=kOutput, calls=%fused_computation.39 | convolution fusion | flops 536870912 | bytes 3670016 | tf_op jit(solution)/shard_map/dot_general | solution.py:43
  165.1 3.2 %fusion.26 = f32[16,64,512]{2,1,0:T(8,128)} fusion(bf16[17,66,512]{2,1,0:T(8,128)(2,1)S(1)} %copy-done.2, bf16[4608,512]{1,0:T(8,128)(2,1)} %param.5), kind=kOutput, calls=%fused_computation.41 | convolution fusion | flops 536870912 | bytes 3670016 | tf_op jit(solution)/shard_map/dot_general | solution.py:43
  168.3 3.1 %fusion.28 = f32[16,64,512]{2,1,0:T(8,128)} fusion(bf16[17,66,512]{2,1,0:T(8,128)(2,1)S(1)} %copy-done.2, bf16[4608,512]{1,0:T(8,128)(2,1)} %param.5), kind=kOutput, calls=%fused_computation.43 | convolution fusion | flops 536870912 | bytes 3670016 | tf_op jit(solution)/shard_map/dot_general | solution.py:43
  171.4 11.0 %all-gather.3.cloned.1.call-done = f32[576,512]{1,0:T(8,128)} async-done(((f32[288,512]{1,0:T(8,128)}), f32[576,512]{1,0:T(8,128)}) %all-gather.3.cloned.1.call-update) | async-done | bytes 1179664 | tf_op jit(solution)/shard_map/all_gather | solution.py:84
  182.3 1.4 reduce_sum.18
  184.5 8.2 %fusion.2 = bf16[16,64,512]{2,1,0:T(8,128)(2,1)} fusion(bf16[16,64,512]{2,1,0:T(8,128)(2,1)} %param.4, f32[16,64,512]{2,1,0:T(8,128)} %fusion.16, f32[16,64,512]{2,1,0:T(8,128)} %fusion.18, f32[16,64,512]{2,1,0:T(8,128)} %fusion.20, f32[16,64,512]{2,1,0:T(8,128)S(1)} %fusion.60, f32[16,64,512]{2,1,0:T(8,128)} %fusion.22, f32[16,64,512]{2,1,0:T(8,128)} %fusion.24, ...), kind=kOutput, calls=%fused_computation.4 | convolution fusion | flops 542638080 | bytes 20447232 | tf_op jit(solution)/shard_map/dot_general | solution.py:43
  192.7 33.7 %psum.7 = f32[]{:T(128)} all-reduce(f32[]{:T(128)} %multiply_reduce_fusion), channel_id=1, replica_groups=mesh['lat'=16,'lon'=2] {'lat'}, use_global_device_ids=true, to_apply=%region_3.0 | all-reduce | flops 1 | bytes 8 | tf_op jit(solution)/shard_map/psum | solution.py:85
  227.1 2.2 multiply_add_fusion
  (37 shorter events, 13.7 us)
Async XLA Ops:
  7.2 8.1 %copy-start = (bf16[16,64,512]{2,1,0:T(8,128)(2,1)S(1)}, bf16[16,64,512]{2,1,0:T(8,128)(2,1)}, u32[]{:S(2)}) copy-start(bf16[16,64,512]{2,1,0:T(8,128)(2,1)} %param.3) | copy-start | bytes 3145732
  7.2 151.2 %reduce-scatter.2.cloned.1.call-start = ((), (), s32[]{:S(2)}) async-start(), calls=%async_computation.1 | async-start | bytes 10027008 | tf_op jit(solution)/shard_map/reduce_scatter | solution.py:83
  8.3 5.2 %collective-permute-start = (bf16[16,1,512]{2,1,0:T(2,128)(2,1)S(1)}, bf16[16,1,512]{2,1,0:T(2,128)(2,1)S(1)}, u32[]{:S(2)}, u32[]{:S(2)}) collective-permute-start(bf16[16,1,512]{2,1,0:T(2,128)(2,1)S(1)} %get-tuple-element.15), channel_id=1, source_target_pairs={{0,1},{1,0},{2,3},{3,2},{4,5},{5,4},{6,7},{7,6},{8,9},{9,8},{10,11... | collective-permute-start | bytes 49160 | tf_op jit(solution)/shard_map/ppermute | solution.py:14
  11.4 3.9 %collective-permute-start.1 = (bf16[16,1,512]{2,1,0:T(2,128)(2,1)S(1)}, bf16[16,1,512]{2,1,0:T(2,128)(2,1)S(1)}, u32[]{:S(2)}, u32[]{:S(2)}) collective-permute-start(bf16[16,1,512]{2,1,0:T(2,128)(2,1)S(1)} %get-tuple-element.16), channel_id=1, source_target_pairs={{1,0},{0,1},{3,2},{2,3},{5,4},{4,5},{7,6},{6,7},{9,8},{8,9},{11,10... | collective-permute-start | bytes 49160 | tf_op jit(solution)/shard_map/ppermute | solution.py:17
  15.3 4.7 %copy-start.4 = (bf16[4608,512]{1,0:T(8,128)(2,1)S(1)}, bf16[4608,512]{1,0:T(8,128)(2,1)}, u32[]{:S(2)}) copy-start(bf16[4608,512]{1,0:T(8,128)(2,1)} %param.5) | copy-start | bytes 14155780
  15.3 5.4 %collective-permute-start.2 = (bf16[1,66,512]{2,1,0:T(8,128)(2,1)S(1)}, bf16[1,66,512]{2,1,0:T(8,128)(2,1)S(1)}, u32[]{:S(2)}, u32[]{:S(2)}) collective-permute-start(bf16[1,66,512]{2,1,0:T(8,128)(2,1)S(1)} %get-tuple-element.11), channel_id=1, source_target_pairs={{0,2},{2,4},{4,6},{6,8},{8,10},{10,12},{12,14},{14,16},{16,18},{18... | collective-permute-start | bytes 202760 | tf_op jit(solution)/shard_map/ppermute | solution.py:14
  16.9 4.9 %collective-permute-start.3 = (bf16[1,66,512]{2,1,0:T(8,128)(2,1)S(1)}, bf16[1,66,512]{2,1,0:T(8,128)(2,1)S(1)}, u32[]{:S(2)}, u32[]{:S(2)}) collective-permute-start(bf16[1,66,512]{2,1,0:T(8,128)(2,1)S(1)} %get-tuple-element.12), channel_id=1, source_target_pairs={{2,0},{4,2},{6,4},{8,6},{10,8},{12,10},{14,12},{16,14},{18,16},{20... | collective-permute-start | bytes 202760 | tf_op jit(solution)/shard_map/ppermute | solution.py:17
  25.4 1.2 copy-start.3
  44.1 138.2 %all-gather.3.cloned.1.call-start = ((), (), s32[]{:S(2)}) async-start(), calls=%async_computation.2 | async-start | bytes 1769472 | tf_op jit(solution)/shard_map/all_gather | solution.py:84
  44.2 4.0 %collective-permute-start.5 = (bf16[16,1,512]{2,1,0:T(2,128)(2,1)S(1)}, bf16[16,1,512]{2,1,0:T(2,128)(2,1)S(1)}, u32[]{:S(2)}, u32[]{:S(2)}) collective-permute-start(bf16[16,1,512]{2,1,0:T(2,128)(2,1)S(1)} %get-tuple-element.14), channel_id=1, source_target_pairs={{1,0},{0,1},{3,2},{2,3},{5,4},{4,5},{7,6},{6,7},{9,8},{8,9},{11,10... | collective-permute-start | bytes 49160 | tf_op jit(solution)/shard_map/ppermute | solution.py:17
  44.8 3.9 %collective-permute-start.4 = (bf16[16,1,512]{2,1,0:T(2,128)(2,1)S(1)}, bf16[16,1,512]{2,1,0:T(2,128)(2,1)S(1)}, u32[]{:S(2)}, u32[]{:S(2)}) collective-permute-start(bf16[16,1,512]{2,1,0:T(2,128)(2,1)S(1)} %get-tuple-element.13), channel_id=1, source_target_pairs={{0,1},{1,0},{2,3},{3,2},{4,5},{5,4},{6,7},{7,6},{8,9},{9,8},{10,11... | collective-permute-start | bytes 49160 | tf_op jit(solution)/shard_map/ppermute | solution.py:14
  48.8 12.2 %collective-permute-start.6 = (bf16[1,66,512]{2,1,0:T(8,128)(2,1)S(1)}, bf16[1,66,512]{2,1,0:T(8,128)(2,1)S(1)}, u32[]{:S(2)}, u32[]{:S(2)}) collective-permute-start(bf16[1,66,512]{2,1,0:T(8,128)(2,1)S(1)} %get-tuple-element.7), channel_id=1, source_target_pairs={{2,0},{4,2},{6,4},{8,6},{10,8},{12,10},{14,12},{16,14},{18,16},{20... | collective-permute-start | bytes 202760 | tf_op jit(solution)/shard_map/ppermute | solution.py:17
  50.1 10.9 %collective-permute-start.7 = (bf16[1,66,512]{2,1,0:T(8,128)(2,1)S(1)}, bf16[1,66,512]{2,1,0:T(8,128)(2,1)S(1)}, u32[]{:S(2)}, u32[]{:S(2)}) collective-permute-start(bf16[1,66,512]{2,1,0:T(8,128)(2,1)S(1)} %get-tuple-element.8), channel_id=1, source_target_pairs={{0,2},{2,4},{4,6},{6,8},{8,10},{10,12},{12,14},{14,16},{16,18},{18... | collective-permute-start | bytes 202760 | tf_op jit(solution)/shard_map/ppermute | solution.py:14
  62.8 1.1 copy-start.1
  158.4 3.6 %copy-start.2 = (bf16[17,66,512]{2,1,0:T(8,128)(2,1)S(1)}, bf16[17,66,512]{2,1,0:T(8,128)(2,1)}, u32[]{:S(2)}) copy-start(bf16[17,66,512]{2,1,0:T(8,128)(2,1)} %get-tuple-element.5) | copy-start | bytes 3446788
Sparse Core Ops, SparseCore 0:
  44.3 114.0 reduce-scatter.1
  159.9 22.3 all-gather.2
